TPU v7x, 32 devices: a whole 2x2x4 slice. The times are simulated.
32 devices in a mesh: dp: 8 (over y, x, core), mp: 4 (over z).
Axes of the slice: x: 2, y: 2, z: 4, core: 2. Of those that a mesh axis runs over, the one named last changes fastest.
Arguments:
- vit_features: bfloat16 [32, 256, 1024], P('dp', 'mp'), may hold values from -6 to 6
- patch_counts: int32 [32], P('dp'), may hold values from 64 to 192
- text_counts: int32 [32], P('dp'), may hold values from 1 to 63
- tile_dest: int32 [32], P('dp'), may hold values from 0 to 7, as said below
- text_embeds: bfloat16 [32, 256, 4096], P('dp', 'mp'), may hold values from -6 to 6
- w_proj: bfloat16 [1024, 4096], replicated, may hold values from -0.1875 to 0.1875
- b_proj: float32 [4096], replicated, may hold values from -3 to 3
- norm_gain: float32 [1, 4096], replicated, may hold values from 0.1 to 1.9
- w_qkv: bfloat16 [1, 4096, 8, 512], P(None, 'dp', 'mp'), may hold values from -0.375 to 0.375
- w_out: bfloat16 [1, 8, 256, 4096], P(None, 'mp', None, 'dp'), may hold values from -0.125 to 0.125
Outputs:
- hidden_out: bfloat16 [32, 256, 4096], P('dp', 'mp')
Inputs may be any that keep to these rules, and one draw needn't show every extreme that they name: `tile_dest`: each language-model rank receives exactly 4 tiles; one source rank sends at most 2 tiles to one language-model rank, and every source rank sends 2 to some rank.
All inputs are finite; a program needn't handle non-finite values.
Results may differ from a plain program's by a relative error of at most 0.01.
Values may be sent and summed in bfloat16 or wider, within the bound.
A program may use at most 128 MiB of HBM per device.

v0:
```python
import math
import jax
import jax.numpy as jnp
from jax import lax
from jax.sharding import PartitionSpec as P

HS = 128
GROUP = 2
CAP = 2
rope_base = 500000.0
epsilon = 1e-05


def tile_angles(tile_size, head_size):
    half_size = head_size // 2
    inverse = jnp.exp(
        -(2.0 * jnp.arange(half_size, dtype=jnp.float32) / head_size) * math.log(rope_base)
    )
    positions = jnp.arange(tile_size, dtype=jnp.float32)
    return positions[:, None] * inverse[None, :]


def rotate_half(values, angles):
    half_size = values.shape[-1] // 2
    cosine = jnp.cos(angles)
    sine_part = jnp.sin(angles)
    first_half = values[..., :half_size]
    second = values[..., half_size:]
    return jnp.concatenate(
        [first_half * cosine - second * sine_part, second * cosine + first_half * sine_part],
        axis=-1,
    )


def slot_table(full_dest, dest_ids):
    full_hot = (full_dest[:, None] == dest_ids[None, :]).astype(jnp.int32)
    return jnp.sum((jnp.cumsum(full_hot, axis=0) - full_hot) * full_hot, axis=1)


def send_capped(vit_features, tile_dest, own_before, full_dest, full_slots, rank_count, my_rank):
    image_count, local_rows, vision_width = vit_features.shape
    targets = tile_dest * CAP + own_before
    placing = (targets[:, None] == jnp.arange(rank_count * CAP, dtype=jnp.int32)[None, :]).astype(
        jnp.bfloat16
    )
    flat_rows = vit_features.reshape(image_count, local_rows * vision_width)
    outgoing = jnp.dot(placing.T, flat_rows, preferred_element_type=jnp.float32).astype(
        jnp.bfloat16
    )
    outgoing = outgoing.reshape(rank_count, CAP, local_rows, vision_width)
    incoming = lax.all_to_all(outgoing, "dp", split_axis=0, concat_axis=0, tiled=True)
    image_total = full_dest.shape[0]
    dest_ids = jnp.arange(rank_count, dtype=jnp.int32)
    by_source = full_dest.reshape(rank_count, image_count)
    source_hot = (by_source[:, :, None] == dest_ids[None, None, :]).astype(jnp.int32)
    source_before = jnp.sum(
        (jnp.cumsum(source_hot, axis=1) - source_hot) * source_hot, axis=2
    ).reshape(image_total)
    columns = jnp.arange(image_total, dtype=jnp.int32) // image_count * CAP + source_before
    mine_mask = full_dest == my_rank
    pick_rows = (
        mine_mask[None, :]
        & (full_slots[None, :] == jnp.arange(image_count, dtype=jnp.int32)[:, None])
    ).astype(jnp.bfloat16)
    pick_cols = (columns[:, None] == jnp.arange(rank_count * CAP, dtype=jnp.int32)[None, :]).astype(
        jnp.bfloat16
    )
    selector = jnp.dot(pick_rows, pick_cols, preferred_element_type=jnp.float32).astype(
        jnp.bfloat16
    )
    arrived = jnp.dot(
        selector,
        incoming.reshape(rank_count * CAP, local_rows * vision_width),
        preferred_element_type=jnp.float32,
    )
    return arrived.astype(jnp.bfloat16).reshape(image_count, local_rows, vision_width)


def layer_step(hidden, gain_row, weights_qkv, weights_out, lengths, angles):
    as_float = hidden.astype(jnp.float32)
    mean_square = jnp.mean(as_float * as_float, axis=-1, keepdims=True)
    normed = (as_float * lax.rsqrt(mean_square + epsilon) * gain_row).astype(jnp.bfloat16)
    full_rows = lax.all_gather(normed, "mp", axis=1, tiled=True)
    image_count, tile_size, model_width = full_rows.shape
    head_count = weights_qkv.shape[1]
    joined_rows = jnp.dot(
        full_rows.reshape(image_count * tile_size, model_width),
        weights_qkv.reshape(model_width, -1),
        preferred_element_type=jnp.float32,
    )
    joined_rows = joined_rows.reshape(image_count, tile_size, head_count, GROUP + 2, HS)
    queries = rotate_half(joined_rows[:, :, :, :GROUP, :], angles[None, :, None, None, :]).astype(
        jnp.bfloat16
    )
    key_heads = rotate_half(joined_rows[:, :, :, GROUP, :], angles[None, :, None, :]).astype(
        jnp.bfloat16
    )
    value_heads = joined_rows[:, :, :, GROUP + 1, :].astype(jnp.bfloat16)
    score_scale = 1.0 / math.sqrt(HS)
    scores = (
        jnp.einsum("brhge,bche->bhgrc", queries, key_heads, preferred_element_type=jnp.float32)
        * score_scale
    )
    row_ids = jnp.arange(tile_size, dtype=jnp.int32)[:, None]
    col_ids = jnp.arange(tile_size, dtype=jnp.int32)[None, :]
    allowed = (col_ids <= row_ids)[None, None, None, :, :] & (
        col_ids[None, None, None, :, :] < lengths[:, None, None, None, None]
    )
    scores = jnp.where(allowed, scores, -1e30)
    row_max = jnp.max(scores, axis=-1, keepdims=True)
    weights = jnp.where(allowed, jnp.exp(scores - row_max), 0.0)
    probabilities = (weights / jnp.sum(weights, axis=-1, keepdims=True)).astype(jnp.bfloat16)
    attended = jnp.einsum(
        "bhgrc,bche->brhge", probabilities, value_heads, preferred_element_type=jnp.float32
    ).astype(jnp.bfloat16)
    head_term = jnp.dot(
        attended.reshape(image_count * tile_size, -1),
        weights_out.reshape(-1, model_width),
        preferred_element_type=jnp.float32,
    )
    head_term = head_term.reshape(image_count, tile_size, model_width)
    summed = lax.psum_scatter(
        head_term.astype(jnp.bfloat16), "mp", scatter_dimension=1, tiled=True
    ).astype(jnp.float32)
    return (as_float + summed).astype(jnp.bfloat16)


def body(
    vit_features,
    patch_counts,
    text_counts,
    tile_dest,
    text_embeds,
    w_proj,
    b_proj,
    norm_gain,
    w_qkv,
    w_out,
):
    rank_count = lax.axis_size("dp")
    my_rank = lax.axis_index("dp")
    image_count, local_rows, vision_width = vit_features.shape
    dest_ids = jnp.arange(rank_count, dtype=jnp.int32)
    own_hot = (tile_dest[:, None] == dest_ids[None, :]).astype(jnp.int32)
    own_before = jnp.sum((jnp.cumsum(own_hot, axis=0) - own_hot) * own_hot, axis=1)
    full_dest = lax.all_gather(tile_dest, "dp", axis=0, tiled=True)
    full_slots = slot_table(full_dest, dest_ids)
    arrived = send_capped(
        vit_features, tile_dest, own_before, full_dest, full_slots, rank_count, my_rank
    )
    mp_rank = lax.axis_index("mp")
    projected = (
        jnp.dot(
            arrived.reshape(image_count * local_rows, vision_width),
            w_proj,
            preferred_element_type=jnp.float32,
        )
        + b_proj
    )
    projected = projected.reshape(image_count, local_rows, -1)
    row_ids = (mp_rank * local_rows + jnp.arange(local_rows, dtype=jnp.int32))[None, :, None]
    image_end = patch_counts[:, None, None]
    text_end = (patch_counts + text_counts)[:, None, None]
    hidden = jnp.where(
        row_ids < image_end,
        projected,
        jnp.where(row_ids < text_end, text_embeds.astype(jnp.float32), 0.0),
    ).astype(jnp.bfloat16)
    lengths = patch_counts + text_counts
    all_qkv, all_out = (
        lax.all_gather(w_qkv, "dp", axis=1, tiled=True),
        lax.all_gather(w_out, "dp", axis=3, tiled=True),
    )
    tile_size = local_rows * lax.axis_size("mp")
    angles = tile_angles(tile_size, HS)
    hidden = layer_step(hidden, norm_gain[0], all_qkv[0], all_out[0], lengths, angles)
    return hidden


def solution(mesh):
    in_specs = (
        P("dp", "mp", None),
        P("dp"),
        P("dp"),
        P("dp"),
        P("dp", "mp", None),
        P(),
        P(),
        P(),
        P(None, "dp", "mp", None),
        P(None, "mp", None, "dp"),
    )
    out_specs = P("dp", "mp", None)
    return jax.shard_map(body, mesh=mesh, in_specs=in_specs, out_specs=out_specs, check_vma=False)
```

profile of v0, /device:TPU:0, one launch (start us, length us, event | category | flops | bytes accessed | tf_op | source)
XLA Modules:
  0.0 441.3 jit_solution(15001125741120260117)
XLA Ops:
  6.5 0.0 all-gather.6.cloned.1.call-start
  6.5 0.7 all-gather.6.cloned.1.call-update
  7.3 1.4 copy.44
  8.7 0.7 fusion.29
  9.5 0.8 select_reduce_fusion.1
  10.3 0.7 multiply_add_fusion
  11.0 0.9 convolution_convert_fusion
  11.8 0.0 copy-start.6
  11.8 0.0 copy-start.2
  11.9 0.0 copy-start.3
  11.9 0.0 copy-start.5
  11.9 2.5 copy.45
  14.4 5.2 %all-to-all-start = ((bf16[8,2,64,1024]{3,2,1,0:T(8,128)(2,1)}), bf16[8,2,64,1024]{3,2,1,0:T(8,128)(2,1)S(1)}, u32[]{:S(2)}, u32[]{:S(2)}) async-start(bf16[8,2,64,1024]{3,2,1,0:T(8,128)(2,1)} %bitcast.63), calls=%async_computation | async-start | bytes 4194304 | tf_op jit(solution)/shard_map/all_to_all | solution.py:51
  19.6 0.0 all-gather.4.cloned.1.call-start
  19.6 0.0 copy-done.6
  19.6 0.6 dynamic-slice
  20.8 0.0 copy-done.2
  20.8 0.2 dynamic-update-slice
  21.0 38.3 %all-reduce = s32[32]{0:T(128)S(1)} all-reduce(s32[32]{0:T(128)S(1)} %dynamic-update-slice), channel_id=1, replica_groups=mesh['dp'=8,'mp'=4] {'dp'}, use_global_device_ids=true, to_apply=%add | all-reduce | flops 32 | bytes 256
  59.3 0.1 eq.94
  59.4 0.1 copy.27
  59.5 0.2 fusion.43
  59.7 0.1 copy.28
  59.8 0.1 reshape.260
  59.9 0.1 fusion.25
  59.9 0.1 reduce_window_sum.33
  60.0 0.0 copy-done.3
  60.0 0.0 copy-done.5
  60.0 0.2 select_reduce_fusion
  60.2 0.1 broadcast_compare_fusion.1
  60.3 0.0 all-to-all-done
  60.3 2.6 copy.46
  62.9 2.8 convolution_convert_fusion.1
  65.7 0.4 reshape_reshape.3
  66.1 0.0 copy-done.4
  66.1 0.0 copy-start
  66.2 5.9 %convolution_add_fusion = bf16[256,4096]{1,0:T(8,128)(2,1)S(1)} fusion(bf16[256,1024]{1,0:T(8,128)(2,1)S(1)} %reshape_reshape.3, bf16[1024,4096]{1,0:T(8,128)(2,1)} %param.15, f32[4096]{0:T(1024)S(1)} %copy-done.4), kind=kOutput, calls=%fused_computation.9 | convolution fusion | flops 2149580800 | bytes 11026432 | tf_op jit(solution)/shard_map/dot_general | solution.py:153
  72.1 0.0 copy-start.1
  72.1 0.0 copy-done
  72.1 1.0 fusion.3
  73.2 0.0 copy-done.1
  73.2 2.0 fusion.5
  75.1 0.0 all-gather.4.cloned.1.call-update
  75.1 0.0 all-gather.8.cloned.1.call-start
  75.2 0.7 all-gather.8.cloned.1.call-update
  75.9 0.2 reduce-scatter.2.cloned.1.call-start
  76.2 0.1 iota_compare_fusion.7
  76.2 0.3 fusion.23
  76.5 0.2 broadcast_and_fusion
  76.7 12.0 %all-gather.6.cloned.1.call-done = bf16[1,4096,2,512]{3,2,0,1:T(2,128)(2,1)} async-done(((bf16[1,512,2,512]{3,2,0,1:T(2,128)(2,1)}), bf16[1,4096,2,512]{3,2,0,1:T(2,128)(2,1)}) %all-gather.6.cloned.1.call-update) | async-done | bytes 8388624 | tf_op jit(solution)/shard_map/all_gather | solution.py:171
  88.7 21.5 %copy.41 = bf16[1,4096,2,512]{1,3,2,0:T(8,128)(2,1)} copy(bf16[1,4096,2,512]{3,2,0,1:T(2,128)(2,1)} %all-gather.6.cloned.1.call-done) | data formatting | bytes 16777216 | tf_op jit(solution)/shard_map/reshape;squeeze | solution.py:88
  110.2 129.7 %all-gather.4.cloned.1.call-done = bf16[4,256,4096]{2,1,0:T(8,128)(2,1)} async-done(((bf16[4,64,4096]{2,1,0:T(8,128)(2,1)}), bf16[4,256,4096]{2,1,0:T(8,128)(2,1)}) %all-gather.4.cloned.1.call-update) | async-done | bytes 8388624 | tf_op jit(solution)/shard_map/all_gather | solution.py:83
  239.9 12.7 %fusion.1 = f32[4,256,2,4,128]{1,4,3,2,0:T(8,128)S(1)} fusion(bf16[2,4,128,4096,1]{3,2,1,0,4:T(8,128)(2,1)} %bitcast.61, bf16[4,256,4096]{2,1,0:T(8,128)(2,1)} %all-gather.4.cloned.1.call-done), kind=kOutput, calls=%fused_computation.3 | convolution fusion | flops 8589934592 | bytes 20971520 | tf_op jit(solution)/shard_map/dot_general | solution.py:86
  252.6 0.1 slice_bitcast_fusion
  252.7 0.1 subtract_convert_fusion.1
  252.9 0.3 subtract_convert_fusion
  253.2 0.8 fusion.14
  254.0 1.7 fusion.44
  255.7 0.5 fusion.12
  256.2 21.1 %all-gather.8.cloned.1.call-done = bf16[1,2,256,4096]{3,2,1,0:T(8,128)(2,1)} async-done(((bf16[1,2,256,512]{3,2,1,0:T(8,128)(2,1)}), bf16[1,2,256,4096]{3,2,1,0:T(8,128)(2,1)}) %all-gather.8.cloned.1.call-update) | async-done | bytes 4194320 | tf_op jit(solution)/shard_map/all_gather | solution.py:172
  277.4 8.9 %convolution_convert_fusion.2 = bf16[4,256,4096]{2,1,0:T(8,128)(2,1)} fusion(bf16[4,256,512]{1,2,0:T(8,128)(2,1)S(1)} %bitcast.72, bf16[512,4096,1]{1,0,2:T(8,128)(2,1)} %bitcast.71), kind=kOutput, calls=%fused_computation.5 | convolution fusion | flops 4299161600 | bytes 13631488 | tf_op jit(solution)/shard_map/dot_general | solution.py:116
  286.3 0.0 reduce-scatter.2.cloned.1.call-update
  286.3 144.8 %reduce-scatter.2.cloned.1.call-done = bf16[4,64,4096]{2,1,0:T(8,128)(2,1)} async-done(((bf16[4,256,4096]{2,1,0:T(8,128)(2,1)}), bf16[4,64,4096]{2,1,0:T(8,128)(2,1)}) %reduce-scatter.2.cloned.1.call-update) | async-done | bytes 2097168 | tf_op jit(solution)/shard_map/reduce_scatter | solution.py:122
  431.1 3.7 fusion.6
  (10 shorter events, 0.1 us)
Async XLA Ops:
  6.5 82.2 %all-gather.6.cloned.1.call-start = ((), (), s32[]{:S(2)}) async-start(), calls=%async_computation.3 | async-start | bytes 9437184 | tf_op jit(solution)/shard_map/all_gather | solution.py:171
  11.8 7.8 %copy-start.6 = (u32[32]{0:T(128)S(1)}, u32[32]{0:T(128)}, u32[]{:S(2)}) copy-start(u32[32]{0:T(128)} %constant.73) | copy-start | bytes 388
  11.8 8.9 %copy-start.2 = (s32[4]{0:T(128)S(1)}, s32[4]{0:T(128)}, u32[]{:S(2)}) copy-start(s32[4]{0:T(128)} %param.13) | copy-start | bytes 52
  11.9 48.1 %copy-start.3 = (s32[4]{0:T(128)S(1)}, s32[4]{0:T(128)}, u32[]{:S(2)}) copy-start(s32[4]{0:T(128)} %param.11) | copy-start | bytes 52
  11.9 48.1 %copy-start.5 = (s32[4]{0:T(128)S(1)}, s32[4]{0:T(128)}, u32[]{:S(2)}) copy-start(s32[4]{0:T(128)} %param.12) | copy-start | bytes 52
  14.4 46.0 %all-to-all-start = ((bf16[8,2,64,1024]{3,2,1,0:T(8,128)(2,1)}), bf16[8,2,64,1024]{3,2,1,0:T(8,128)(2,1)S(1)}, u32[]{:S(2)}, u32[]{:S(2)}) async-start(bf16[8,2,64,1024]{3,2,1,0:T(8,128)(2,1)} %bitcast.63), calls=%async_computation | async-start | bytes 4194304 | tf_op jit(solution)/shard_map/all_to_all | solution.py:51
  19.6 46.6 %copy-start.4 = (f32[4096]{0:T(1024)S(1)}, f32[4096]{0:T(1024)}, u32[]{:S(2)}) copy-start(f32[4096]{0:T(1024)} %param.16) | copy-start | bytes 49156
  19.6 220.3 %all-gather.4.cloned.1.call-start = ((), (), s32[]{:S(2)}) async-start(), calls=%async_computation.2 | async-start | bytes 10485760 | tf_op jit(solution)/shard_map/all_gather | solution.py:83
  66.1 5.9 %copy-start = (bf16[4,64,4096]{2,1,0:T(8,128)(2,1)S(1)}, bf16[4,64,4096]{2,1,0:T(8,128)(2,1)}, u32[]{:S(2)}) copy-start(bf16[4,64,4096]{2,1,0:T(8,128)(2,1)} %param.14) | copy-start | bytes 6291460
  72.1 1.1 copy-start.1
  75.1 202.2 %all-gather.8.cloned.1.call-start = ((), (), s32[]{:S(2)}) async-start(), calls=%async_computation.4 | async-start | bytes 4718592 | tf_op jit(solution)/shard_map/all_gather | solution.py:172
  75.9 355.2 %reduce-scatter.2.cloned.1.call-start = ((), (), s32[]{:S(2)}) async-start(), calls=%async_computation.5 | async-start | bytes 10485760 | tf_op jit(solution)/shard_map/reduce_scatter | solution.py:122
Sparse Core Ops, SparseCore 0:
  9.2 79.4 all-gather.5
  90.3 149.5 all-gather.3
  241.8 35.5 all-gather.7
  286.4 144.6 reduce-scatter.1
where the time goes:
time: 442 us; the launch traced here: 441 us
  waiting for transfers between devices  309 us (70%)
  blocking collectives  38.3 us (9%)
  matrix products  32.5 us (7%)
  local copies, waits for them, and re-layouts  29.7 us (7%)
  between operations  13.9 us (3%)
  other arithmetic  12.4 us (3%)
  starting transfers between devices  5.51 us (1%)
    reduce_scatter x1, waiting for transfers between devices, layer_step(): lax.psum_scatter(head_term.astype(jnp.bfloat16), 'mp', scatter_dimension=...  145 us
    all_gather x1, waiting for transfers between devices, layer_step(): full_rows = lax.all_gather(normed, 'mp', axis=1, tiled=True)  130 us
    unnamed x1, blocking collectives  38.3 us
    another operation x1, local copies, waits for them, and re-layouts, layer_step(): weights_qkv.reshape(model_width, -1)  21.5 us
    all_gather x1, waiting for transfers between devices, body(): lax.all_gather(w_out, 'dp', axis=3, tiled=True)  21.1 us
    dot_general x1, matrix products, layer_step(): jnp.dot(full_rows.reshape(image_count * tile_size, model_width), weights_...  12.7 us
    all_gather x1, waiting for transfers between devices, body(): lax.all_gather(w_qkv, 'dp', axis=1, tiled=True)  12 us
    dot_general x1, matrix products, layer_step(): jnp.dot(attended.reshape(image_count * tile_size, -1), weights_out.reshap...  8.92 us
  transfers between devices with their start and end apart: 5, of which 4 were waited for; matrix products, arithmetic and copies ran while one was open for 14% of the time, Pallas kernels for 0%

commit v1 on v0

--- a/solution.py
+++ b/solution.py
@@ -80,7 +80,7 @@
     as_float = hidden.astype(jnp.float32)
     mean_square = jnp.mean(as_float * as_float, axis=-1, keepdims=True)
     normed = (as_float * lax.rsqrt(mean_square + epsilon) * gain_row).astype(jnp.bfloat16)
-    full_rows = lax.all_gather(normed, "mp", axis=1, tiled=True)
+    full_rows = jnp.concatenate(lax.all_gather(normed, "mp"), axis=1)
     image_count, tile_size, model_width = full_rows.shape
     head_count = weights_qkv.shape[1]
     joined_rows = jnp.dot(

time: 442 us -> 470 us (1.063)
  waiting for transfers between devices: 309 us -> 341 us
  blocking collectives: 38.3 us -> 27.2 us
  local copies, waits for them, and re-layouts: 29.7 us -> 37.3 us
    all_gather x1, waiting for transfers between devices: 12 us -> 46.4 us  [body(): lax.all_gather(w_qkv, 'dp', axis=1, tiled=True)]
    all_gather x1, waiting for transfers between devices: 21.1 us -> 1.28 us  [body(): lax.all_gather(w_out, 'dp', axis=3, tiled=True)]
    all_gather x1, waiting for transfers between devices: 130 us -> 147 us  [layer_step(): full_rows = jnp.concatenate(lax.all_gather(normed, 'mp'), axis=1)]
    unnamed x1, blocking collectives: 38.3 us -> 27.2 us
    all_gather x0 -> x1, local copies, waits for them, and re-layouts: none -> 7.96 us  [layer_step(): full_rows = jnp.concatenate(lax.all_gather(normed, 'mp'), axis=1)]
  transfers between devices with their start and end apart: 5 -> 5, of which waited for: 4 -> 4; matrix products, arithmetic and copies ran while one was open for 14% -> 10% of each run, Pallas kernels for 0% -> 0%
where the time goes in v1:
time: 470 us
  waiting for transfers between devices  341 us (73%)
  local copies, waits for them, and re-layouts  37.3 us (8%)
  matrix products  32.3 us (7%)
  blocking collectives  27.2 us (6%)
  between operations  14.1 us (3%)
  other arithmetic  12.4 us (3%)
  starting transfers between devices  5.53 us (1%)
    all_gather x1, waiting for transfers between devices, layer_step(): full_rows = jnp.concatenate(lax.all_gather(normed, 'mp'), axis=1)  147 us
    reduce_scatter x1, waiting for transfers between devices, layer_step(): lax.psum_scatter(head_term.astype(jnp.bfloat16), 'mp', scatter_dimension=...  145 us
    all_gather x1, waiting for transfers between devices, body(): lax.all_gather(w_qkv, 'dp', axis=1, tiled=True)  46.4 us
    unnamed x1, blocking collectives  27.2 us
    another operation x1, local copies, waits for them, and re-layouts, layer_step(): weights_qkv.reshape(model_width, -1)  21.2 us
    dot_general x1, matrix products, layer_step(): jnp.dot(full_rows.reshape(image_count * tile_size, model_width), weights_...  13.2 us
  transfers between devices with their start and end apart: 5, of which 4 were waited for; matrix products, arithmetic and copies ran while one was open for 10% of the time, Pallas kernels for 0%

profile of v1, /device:TPU:0, one launch (start us, length us, event | category | flops | bytes accessed | tf_op | source)
XLA Modules:
  0.0 469.5 jit_solution(337209637453096029)
XLA Ops:
  6.5 1.4 copy.48
  8.0 0.7 fusion.27
  8.8 0.8 select_reduce_fusion.1
  9.6 0.7 multiply_add_fusion
  10.3 0.9 convolution_convert_fusion
  11.1 0.0 copy-start.6
  11.1 0.0 copy-start.2
  11.1 0.0 copy-start.3
  11.2 0.0 copy-start.5
  11.2 2.5 copy.49
  13.6 5.2 %all-to-all-start = ((bf16[8,2,64,1024]{3,2,1,0:T(8,128)(2,1)}), bf16[8,2,64,1024]{3,2,1,0:T(8,128)(2,1)S(1)}, u32[]{:S(2)}, u32[]{:S(2)}) async-start(bf16[8,2,64,1024]{3,2,1,0:T(8,128)(2,1)} %bitcast.69), calls=%async_computation | async-start | bytes 4194304 | tf_op jit(solution)/shard_map/all_to_all | solution.py:51
  18.8 0.0 all-gather.9.cloned.1.call-start
  18.9 0.0 copy-done.6
  18.9 0.7 dynamic-slice
  20.3 0.0 copy-done.2
  20.3 0.2 dynamic-update-slice
  20.5 27.2 %all-reduce = s32[32]{0:T(128)S(1)} all-reduce(s32[32]{0:T(128)S(1)} %dynamic-update-slice), channel_id=1, replica_groups=mesh['dp'=8,'mp'=4] {'dp'}, use_global_device_ids=true, to_apply=%add | all-reduce | flops 32 | bytes 256
  47.7 0.1 eq.94
  47.8 0.1 fusion.23
  47.8 0.1 reduce_window_sum.33
  47.9 0.1 copy.30
  48.0 0.2 fusion.41
  48.2 0.1 copy.31
  48.3 0.1 reshape.262
  48.4 0.0 copy-done.3
  48.4 0.0 copy-done.5
  48.4 0.2 select_reduce_fusion
  48.6 0.1 broadcast_compare_fusion.1
  48.7 0.0 all-to-all-done
  48.7 2.5 copy.50
  51.2 2.2 convolution_convert_fusion.1
  53.4 0.4 reshape_reshape.4
  53.8 0.0 copy-done.4
  53.8 0.0 copy-start
  53.8 5.9 %convolution_add_fusion = bf16[256,4096]{1,0:T(8,128)(2,1)S(1)} fusion(bf16[256,1024]{1,0:T(8,128)(2,1)S(1)} %reshape_reshape.4, bf16[1024,4096]{1,0:T(8,128)(2,1)} %param.15, f32[4096]{0:T(1024)S(1)} %copy-done.4), kind=kOutput, calls=%fused_computation.7 | convolution fusion | flops 2149580800 | bytes 11026432 | tf_op jit(solution)/shard_map/dot_general | solution.py:153
  59.7 0.0 copy-start.1
  59.7 0.0 copy-done
  59.7 1.0 fusion.1
  60.8 2.0 fusion.3
  62.8 0.0 all-gather.9.cloned.1.call-update
  62.8 0.0 all-gather.5.cloned.1.call-start
  62.8 0.7 all-gather.5.cloned.1.call-update
  63.5 0.0 all-gather.7.cloned.1.call-start
  63.6 0.7 all-gather.7.cloned.1.call-update
  64.3 0.2 reduce-scatter.2.cloned.1.call-start
  64.5 0.1 iota_compare_fusion.7
  64.6 0.3 fusion.21
  64.9 0.2 broadcast_and_fusion
  65.1 146.8 %all-gather.9.cloned.1.call-done = bf16[16,64,4096]{2,1,0:T(8,128)(2,1)} async-done(((bf16[4,64,4096]{2,1,0:T(8,128)(2,1)}), bf16[16,64,4096]{2,1,0:T(8,128)(2,1)}) %all-gather.9.cloned.1.call-update) | async-done | bytes 8388624 | tf_op jit(solution)/shard_map/all_gather | solution.py:83
  212.0 8.0 %copy.32 = bf16[4,4,64,4096]{3,2,0,1:T(8,128)(2,1)} copy(bf16[4,4,64,4096]{3,2,1,0:T(8,128)(2,1)} %bitcast.65) | data formatting | bytes 16777216 | tf_op jit(solution)/shard_map/all_gather | solution.py:83
  219.9 46.4 %all-gather.5.cloned.1.call-done = bf16[1,4096,2,512]{3,2,0,1:T(2,128)(2,1)} async-done(((bf16[1,512,2,512]{3,2,0,1:T(2,128)(2,1)}), bf16[1,4096,2,512]{3,2,0,1:T(2,128)(2,1)}) %all-gather.5.cloned.1.call-update) | async-done | bytes 8388624 | tf_op jit(solution)/shard_map/all_gather | solution.py:171
  266.3 21.2 %copy.45 = bf16[1,4096,2,512]{1,3,2,0:T(8,128)(2,1)} copy(bf16[1,4096,2,512]{3,2,0,1:T(2,128)(2,1)} %all-gather.5.cloned.1.call-done) | data formatting | bytes 16777216 | tf_op jit(solution)/shard_map/reshape;squeeze | solution.py:88
  287.5 13.2 %fusion.43 = f32[4,256,2,4,128]{1,4,3,2,0:T(8,128)S(1)} fusion(bf16[4,256,4096,1,1]{2,1,4,3,0:T(8,128)(2,1)} %bitcast.66, bf16[2,4,128,4096,1]{3,2,1,0,4:T(8,128)(2,1)} %bitcast.67), kind=kOutput, calls=%fused_computation.80 | convolution fusion | flops 8589934592 | bytes 20971520 | tf_op jit(solution)/shard_map/dot_general | solution.py:86
  300.7 0.1 slice_bitcast_fusion
  300.8 0.1 subtract_convert_fusion.1
  301.0 0.3 subtract_convert_fusion
  301.3 0.8 fusion.12
  302.1 1.7 fusion.42
  303.8 0.5 fusion.10
  304.3 1.3 all-gather.7.cloned.1.call-done
  305.6 8.9 %convolution_convert_fusion.2 = bf16[4,256,4096]{2,1,0:T(8,128)(2,1)} fusion(bf16[4,256,512]{1,2,0:T(8,128)(2,1)S(1)} %bitcast.78, bf16[512,4096,1]{1,0,2:T(8,128)(2,1)} %bitcast.77), kind=kOutput, calls=%fused_computation.3 | convolution fusion | flops 4299161600 | bytes 13631488 | tf_op jit(solution)/shard_map/dot_general | solution.py:116
  314.5 0.0 reduce-scatter.2.cloned.1.call-update
  314.5 144.8 %reduce-scatter.2.cloned.1.call-done = bf16[4,64,4096]{2,1,0:T(8,128)(2,1)} async-done(((bf16[4,256,4096]{2,1,0:T(8,128)(2,1)}), bf16[4,64,4096]{2,1,0:T(8,128)(2,1)}) %reduce-scatter.2.cloned.1.call-update) | async-done | bytes 2097168 | tf_op jit(solution)/shard_map/reduce_scatter | solution.py:122
  459.3 3.7 fusion.4
  (11 shorter events, 0.1 us)
Async XLA Ops:
  11.1 7.8 %copy-start.6 = (u32[32]{0:T(128)S(1)}, u32[32]{0:T(128)}, u32[]{:S(2)}) copy-start(u32[32]{0:T(128)} %constant.73) | copy-start | bytes 388
  11.1 9.2 %copy-start.2 = (s32[4]{0:T(128)S(1)}, s32[4]{0:T(128)}, u32[]{:S(2)}) copy-start(s32[4]{0:T(128)} %param.13) | copy-start | bytes 52
  11.1 37.2 %copy-start.3 = (s32[4]{0:T(128)S(1)}, s32[4]{0:T(128)}, u32[]{:S(2)}) copy-start(s32[4]{0:T(128)} %param.11) | copy-start | bytes 52
  11.2 37.2 %copy-start.5 = (s32[4]{0:T(128)S(1)}, s32[4]{0:T(128)}, u32[]{:S(2)}) copy-start(s32[4]{0:T(128)} %param.12) | copy-start | bytes 52
  13.6 35.1 %all-to-all-start = ((bf16[8,2,64,1024]{3,2,1,0:T(8,128)(2,1)}), bf16[8,2,64,1024]{3,2,1,0:T(8,128)(2,1)S(1)}, u32[]{:S(2)}, u32[]{:S(2)}) async-start(bf16[8,2,64,1024]{3,2,1,0:T(8,128)(2,1)} %bitcast.69), calls=%async_computation | async-start | bytes 4194304 | tf_op jit(solution)/shard_map/all_to_all | solution.py:51
  18.8 35.0 %copy-start.4 = (f32[4096]{0:T(1024)S(1)}, f32[4096]{0:T(1024)}, u32[]{:S(2)}) copy-start(f32[4096]{0:T(1024)} %param.16) | copy-start | bytes 49156
  18.8 193.1 %all-gather.9.cloned.1.call-start = ((), (), s32[]{:S(2)}) async-start(), calls=%async_computation.5 | async-start | bytes 10485760 | tf_op jit(solution)/shard_map/all_gather | solution.py:83
  53.8 5.9 %copy-start = (bf16[4,64,4096]{2,1,0:T(8,128)(2,1)S(1)}, bf16[4,64,4096]{2,1,0:T(8,128)(2,1)}, u32[]{:S(2)}) copy-start(bf16[4,64,4096]{2,1,0:T(8,128)(2,1)} %param.14) | copy-start | bytes 6291460
  59.7 1.1 copy-start.1
  62.8 203.5 %all-gather.5.cloned.1.call-start = ((), (), s32[]{:S(2)}) async-start(), calls=%async_computation.2 | async-start | bytes 9437184 | tf_op jit(solution)/shard_map/all_gather | solution.py:171
  63.5 242.1 %all-gather.7.cloned.1.call-start = ((), (), s32[]{:S(2)}) async-start(), calls=%async_computation.3 | async-start | bytes 4718592 | tf_op jit(solution)/shard_map/all_gather | solution.py:172
  64.3 395.0 %reduce-scatter.2.cloned.1.call-start = ((), (), s32[]{:S(2)}) async-start(), calls=%async_computation.4 | async-start | bytes 10485760 | tf_op jit(solution)/shard_map/reduce_scatter | solution.py:122
Sparse Core Ops, SparseCore 0:
  62.9 149.0 all-gather.8
  213.8 52.4 all-gather.4
  268.2 37.3 all-gather.6
  314.7 144.6 reduce-scatter.1
